TPU v7x, 256 devices: a whole 4x4x8 slice. The times are simulated.
256 devices in a mesh: data: 32 (over z, y_hi, core), width: 8 (over y_lo, x).
Axes of the slice: x: 4, y: 4 (y_hi: 2, y_lo: 2; y = y_hi * 2 + y_lo), z: 8, core: 2. Of those that a mesh axis runs over, the one named last changes fastest.
Arguments:
- slope_up: float32 [32, 1280, 5120], P('data', None, 'width'), may hold values from -1.25 to 1.25
- slope_down: float32 [32, 5120, 1280], P('data', 'width'), may hold values from -1.25 to 1.25
- slope_query: float32 [32, 1280, 1280], P('data', None, 'width'), may hold values from -1.25 to 1.25
- slope_key: float32 [32, 1280, 1280], P('data', None, 'width'), may hold values from -1.25 to 1.25
- slope_value: float32 [32, 1280, 1280], P('data', None, 'width'), may hold values from -1.25 to 1.25
- slope_mixed: float32 [32, 1280, 1280], P('data', 'width'), may hold values from -1.25 to 1.25
- slope_norm: float32 [32, 1280], P('data'), may hold values from -12 to 12
- slope_bias: float32 [32, 1280], P('data'), may hold values from -12 to 12
- param_up: float32 [1280, 5120], P('data', 'width'), may hold values from -0.15625 to 0.15625
- param_down: float32 [5120, 1280], P('width', 'data'), may hold values from -0.078125 to 0.078125
- param_query: float32 [1280, 1280], P('data', 'width'), may hold values from -0.15625 to 0.15625
- param_key: float32 [1280, 1280], P('data', 'width'), may hold values from -0.15625 to 0.15625
- param_value: float32 [1280, 1280], P('data', 'width'), may hold values from -0.15625 to 0.15625
- param_mixed: float32 [1280, 1280], P('width', 'data'), may hold values from -0.15625 to 0.15625
- param_norm: float32 [1280], P('data'), may hold values from 0.25 to 1.75
- param_bias: float32 [1280], P('data'), may hold values from -3 to 3
- state_up: float32 [1280, 5120], P('data', 'width'), may hold values from -1.75 to 1.75
- state_down: float32 [5120, 1280], P('width', 'data'), may hold values from -1.75 to 1.75
- state_query: float32 [1280, 1280], P('data', 'width'), may hold values from -1.75 to 1.75
- state_key: float32 [1280, 1280], P('data', 'width'), may hold values from -1.75 to 1.75
- state_value: float32 [1280, 1280], P('data', 'width'), may hold values from -1.75 to 1.75
- state_mixed: float32 [1280, 1280], P('width', 'data'), may hold values from -1.75 to 1.75
- state_norm: float32 [1280], P('data'), may hold values from -1.75 to 1.75
- state_bias: float32 [1280], P('data'), may hold values from -1.75 to 1.75
Outputs:
- half_up: bfloat16 [1280, 5120], P(None, 'width')
- half_down: bfloat16 [5120, 1280], P('width')
- half_query: bfloat16 [1280, 1280], P(None, 'width')
- half_key: bfloat16 [1280, 1280], P(None, 'width')
- half_value: bfloat16 [1280, 1280], P(None, 'width')
- half_mixed: bfloat16 [1280, 1280], P('width')
- half_norm: bfloat16 [1280], replicated
- half_bias: bfloat16 [1280], replicated
- next_up: float32 [1280, 5120], P('data', 'width')
- next_down: float32 [5120, 1280], P('width', 'data')
- next_query: float32 [1280, 1280], P('data', 'width')
- next_key: float32 [1280, 1280], P('data', 'width')
- next_value: float32 [1280, 1280], P('data', 'width')
- next_mixed: float32 [1280, 1280], P('width', 'data')
- next_norm: float32 [1280], P('data')
- next_bias: float32 [1280], P('data')
- state_new_up: float32 [1280, 5120], P('data', 'width')
- state_new_down: float32 [5120, 1280], P('width', 'data')
- state_new_query: float32 [1280, 1280], P('data', 'width')
- state_new_key: float32 [1280, 1280], P('data', 'width')
- state_new_value: float32 [1280, 1280], P('data', 'width')
- state_new_mixed: float32 [1280, 1280], P('width', 'data')
- state_new_norm: float32 [1280], P('data')
- state_new_bias: float32 [1280], P('data')
All inputs are finite; a program needn't handle non-finite values.
Results may differ from a plain program's by a relative error of at most 0.0085.
Values may be sent and summed in bfloat16 or wider, within the bound.
No kernel may reach another device: no remote copies, remote signals or barrier semaphores. Data moves between devices by JAX's collectives and lax.ppermute only.
A program may use at most 128 MiB of HBM per device.

v0:
```python
import jax
import jax.numpy as jnp
from jax import lax
from jax.sharding import PartitionSpec as P

learn_rate = 0.1
hold_rate = 0.8


def in_blocks(shard, dim, peers):
    shape = shard.shape
    parts = shard.reshape(*shape[:dim], peers, shape[dim] // peers, *shape[dim + 1 :])
    return jnp.moveaxis(parts, dim, 0)


def sum_together(arrays, axis, dims):
    peers = lax.axis_size(axis)
    parts = [in_blocks(a, dim, peers) for a, dim in zip(arrays, dims)]
    lines = jnp.concatenate([b.reshape(peers, -1) for b in parts], axis=1)
    extent = max(16, -(-lines.shape[1] // 1024) * 8)
    lines = jnp.pad(lines, ((0, 0), (0, extent * 128 - lines.shape[1]))).reshape(-1, 128)
    vector, at, gathered = (lax.psum_scatter(lines, axis, tiled=True).reshape(-1), 0, [])
    for b in parts:
        part = b[0]
        gathered.append(vector[at : at + part.size].reshape(part.shape))
        at += part.size
    return tuple(gathered)


def turned_gather(arrays, axis, dims):
    turned = [jnp.moveaxis(a, dim, 0) for a, dim in zip(arrays, dims)]
    widths = [t[0].size for t in turned]
    both = jnp.concatenate([t.reshape(-1, w) for t, w in zip(turned, widths)], axis=1)
    whole = lax.all_gather(both, axis, axis=0, tiled=True)
    parts = jnp.split(whole, [sum(widths[:k]) for k in range(1, len(widths))], axis=1)
    return tuple(
        (
            jnp.moveaxis(b.reshape(-1, *t.shape[1:]), 0, dim)
            for b, t, dim in zip(parts, turned, dims)
        )
    )


def on_device(
    slope_up,
    slope_down,
    slope_query,
    slope_key,
    slope_value,
    slope_mixed,
    slope_norm,
    slope_bias,
    param_up,
    param_down,
    param_query,
    param_key,
    param_value,
    param_mixed,
    param_norm,
    param_bias,
    state_up,
    state_down,
    state_query,
    state_key,
    state_value,
    state_mixed,
    state_norm,
    state_bias,
):
    mean_up, mean_down, mean_query, mean_key, mean_value, mean_mixed, mean_norm, mean_bias = (
        sum_together(
            (
                slope_up[0],
                slope_down[0],
                slope_query[0],
                slope_key[0],
                slope_value[0],
                slope_mixed[0],
                slope_norm[0],
                slope_bias[0],
            ),
            "data",
            (0, 1, 0, 0, 0, 1, 0, 0),
        )
    )
    mean_rate = lax.axis_size("data") ** (-0.5)
    mean_up = mean_up * mean_rate
    mean_down = mean_down * mean_rate
    mean_query = mean_query * mean_rate
    mean_key = mean_key * mean_rate
    mean_value = mean_value * mean_rate
    mean_mixed = mean_mixed * mean_rate
    mean_norm = mean_norm * mean_rate
    mean_bias = mean_bias * mean_rate
    state_new_up = hold_rate * state_up + mean_up
    next_up = param_up - learn_rate * state_new_up
    state_new_down = hold_rate * state_down + mean_down
    next_down = param_down - learn_rate * state_new_down
    state_new_query = hold_rate * state_query + mean_query
    next_query = param_query - learn_rate * state_new_query
    state_new_key = hold_rate * state_key + mean_key
    next_key = param_key - learn_rate * state_new_key
    state_new_value = hold_rate * state_value + mean_value
    next_value = param_value - learn_rate * state_new_value
    state_new_mixed = hold_rate * state_mixed + mean_mixed
    next_mixed = param_mixed - learn_rate * state_new_mixed
    state_new_norm = hold_rate * state_norm + mean_norm
    next_norm = param_norm - learn_rate * state_new_norm
    state_new_bias = hold_rate * state_bias + mean_bias
    next_bias = param_bias - learn_rate * state_new_bias
    half_up, half_down, half_query, half_key, half_value, half_mixed, half_norm, half_bias = (
        turned_gather(
            (
                next_up.astype(jnp.bfloat16),
                next_down.astype(jnp.bfloat16),
                next_query.astype(jnp.bfloat16),
                next_key.astype(jnp.bfloat16),
                next_value.astype(jnp.bfloat16),
                next_mixed.astype(jnp.bfloat16),
                next_norm.astype(jnp.bfloat16),
                next_bias.astype(jnp.bfloat16),
            ),
            "data",
            (0, 1, 0, 0, 0, 1, 0, 0),
        )
    )
    return (
        half_up,
        half_down,
        half_query,
        half_key,
        half_value,
        half_mixed,
        half_norm,
        half_bias,
        next_up,
        next_down,
        next_query,
        next_key,
        next_value,
        next_mixed,
        next_norm,
        next_bias,
        state_new_up,
        state_new_down,
        state_new_query,
        state_new_key,
        state_new_value,
        state_new_mixed,
        state_new_norm,
        state_new_bias,
    )


def solution(mesh):
    return jax.shard_map(
        on_device,
        mesh=mesh,
        in_specs=(
            P("data", None, "width"),
            P("data", "width", None),
            P("data", None, "width"),
            P("data", None, "width"),
            P("data", None, "width"),
            P("data", "width", None),
            P("data", None),
            P("data", None),
            P("data", "width"),
            P("width", "data"),
            P("data", "width"),
            P("data", "width"),
            P("data", "width"),
            P("width", "data"),
            P("data"),
            P("data"),
            P("data", "width"),
            P("width", "data"),
            P("data", "width"),
            P("data", "width"),
            P("data", "width"),
            P("width", "data"),
            P("data"),
            P("data"),
        ),
        out_specs=(
            P(None, "width"),
            P("width", None),
            P(None, "width"),
            P(None, "width"),
            P(None, "width"),
            P("width", None),
            P(),
            P(),
            P("data", "width"),
            P("width", "data"),
            P("data", "width"),
            P("data", "width"),
            P("data", "width"),
            P("width", "data"),
            P("data"),
            P("data"),
            P("data", "width"),
            P("width", "data"),
            P("data", "width"),
            P("data", "width"),
            P("data", "width"),
            P("width", "data"),
            P("data"),
            P("data"),
        ),
        check_vma=False,
    )
```

profile of v0, /device:TPU:1, one launch (start us, length us, event | category | flops | bytes accessed | tf_op | source)
XLA Modules:
  0.0 367.7 jit_solution(9540244367930635654)
XLA Ops:
  7.2 3.5 copy.87
  10.7 6.0 %copy.88 = f32[32,640,40]{2,1,0:T(8,128)} copy(f32[32,640,40]{1,2,0:T(8,128)S(1)} %bitcast.19) | data formatting | bytes 6553600 | tf_op jit(solution)/shard_map/transpose | solution.py:13
  16.7 10.0 %reshape.102 = f32[32,25600]{1,0:T(8,128)} reshape(f32[32,640,40]{2,1,0:T(8,128)} %copy.88) | data formatting | bytes 6553600 | tf_op jit(solution)/shard_map/reshape | solution.py:19
  26.7 2.2 reshape_reshape_squeeze.12
  28.9 1.9 constant_dynamic-update-slice_fusion.5
  30.8 2.6 copy.89
  33.4 2.9 reshape_reshape_squeeze.13
  36.4 2.6 copy.90
  39.0 2.8 reshape_reshape_squeeze.14
  41.7 2.6 copy.91
  44.3 2.8 reshape_reshape_squeeze.15
  47.1 2.6 copy.92
  49.7 3.0 copy.93
  52.7 3.8 %reshape.103 = f32[32,6400]{1,0:T(8,128)} reshape(f32[32,160,40]{2,1,0:T(8,128)} %copy.93) | data formatting | bytes 1638400 | tf_op jit(solution)/shard_map/reshape | solution.py:19
  56.8 1.9 constant_dynamic-update-slice_fusion.4
  58.7 2.1 constant_dynamic-update-slice_fusion.3
  60.8 2.1 constant_dynamic-update-slice_fusion.2
  62.9 1.0 constant_dynamic-update-slice_fusion.1
  63.9 0.9 constant_dynamic-update-slice_fusion
  64.8 1.3 dynamic-update-slice.6
  66.1 1.4 dynamic-update-slice.7
  67.5 8.3 %pad.4 = f32[32,77824]{1,0:T(8,128)} pad(f32[32,76880]{1,0:T(8,128)} %dynamic-update-slice.7, f32[]{:T(128)} %constant.5.clone.1), padding=0_0x0_944 | pad | bytes 19802116 | tf_op jit(solution)/shard_map/jit(_pad)/pad | solution.py:21
  75.8 8.2 %reshape.104 = f32[19456,128]{1,0:T(8,128)} reshape(f32[32,77824]{1,0:T(8,128)} %pad.4) | data formatting | bytes 19922944 | tf_op jit(solution)/shard_map/reshape | solution.py:21
  84.2 0.2 all-gather.2.cloned.1.call-start
  84.4 160.1 %reduce-scatter.2.cloned.1.call-done = f32[608,128]{1,0:T(8,128)} async-done(((f32[19456,128]{1,0:T(8,128)}), f32[608,128]{1,0:T(8,128)}) %reduce-scatter.2.cloned.1.call-update) | async-done | bytes 311312 | tf_op jit(solution)/shard_map/reduce_scatter | solution.py:22
  244.6 0.8 slice_multiply_fusion.2
  245.6 0.1 mul.141
  245.9 1.4 convert_bitcast_fusion.2
  247.3 0.1 copy.96
  247.4 0.1 copy.97
  247.5 1.0 slice_multiply_fusion
  248.4 0.2 mul.123
  248.7 0.1 copy.94
  248.9 0.6 convert_bitcast_fusion.1
  249.5 0.6 fusion.6
  250.2 0.7 convert_bitcast_fusion
  250.9 0.7 fusion.7
  251.6 0.7 fusion.4
  252.3 0.8 concatenate.7
  253.1 93.3 %all-gather.2.cloned.1.call-done = bf16[1280,1922]{1,0:T(8,128)(2,1)} async-done(((bf16[40,1922]{1,0:T(8,128)(2,1)}), bf16[1280,1922]{1,0:T(8,128)(2,1)}) %all-gather.2.cloned.1.call-update) | async-done | bytes 4920336 | tf_op jit(solution)/shard_map/all_gather | solution.py:34
  346.4 3.1 slice_bitcast_fusion.1
  349.4 1.0 copy.100
  350.4 1.0 copy.101
  351.4 1.0 copy.102
  352.3 1.0 copy.99
  353.3 3.4 slice_bitcast_fusion
  356.7 2.2 copy.98
  358.8 2.0 slice_reduce_fusion
  (54 shorter events, 0.7 us)
Async XLA Ops:
  7.2 237.4 %reduce-scatter.2.cloned.1.call-start = ((), (), s32[]{:S(2)}) async-start(), calls=%async_computation.1 | async-start | bytes 10272768 | tf_op jit(solution)/shard_map/reduce_scatter | solution.py:22
  33.4 23.1 %copy-start.15 = (f32[1,1280]{1,0:T(1,128)S(1)}, f32[1,1280]{1,0:T(1,128)}, u32[]{:S(2)}) copy-start(f32[1,1280]{1,0:T(1,128)} %param.30) | copy-start | bytes 15364
  33.4 23.2 %copy-start.16 = (f32[1,1280]{1,0:T(1,128)S(1)}, f32[1,1280]{1,0:T(1,128)}, u32[]{:S(2)}) copy-start(f32[1,1280]{1,0:T(1,128)} %param.31) | copy-start | bytes 15364
  33.4 23.3 %copy-start = (f32[32,25600]{1,0:T(8,128)S(1)}, f32[32,25600]{1,0:T(8,128)}, u32[]{:S(2)}) copy-start(f32[32,25600]{1,0:T(8,128)} %reshape.102) | copy-start | bytes 9830404
  56.7 6.1 %copy-start.1 = (f32[32,6400]{1,0:T(8,128)S(1)}, f32[32,6400]{1,0:T(8,128)}, u32[]{:S(2)}) copy-start(f32[32,6400]{1,0:T(8,128)} %reshape_reshape_squeeze.15) | copy-start | bytes 2457604
  56.8 7.1 %copy-start.2 = (f32[32,6400]{1,0:T(8,128)S(1)}, f32[32,6400]{1,0:T(8,128)}, u32[]{:S(2)}) copy-start(f32[32,6400]{1,0:T(8,128)} %reshape.103) | copy-start | bytes 2457604
  84.0 161.9 %copy-start.17 = (f32[40]{0:T(128)S(1)}, f32[40]{0:T(128)}, u32[]{:S(2)}) copy-start(f32[40]{0:T(128)} %param.39) | copy-start | bytes 484
  84.0 161.9 %copy-start.18 = (f32[40]{0:T(128)S(1)}, f32[40]{0:T(128)}, u32[]{:S(2)}) copy-start(f32[40]{0:T(128)} %param.47) | copy-start | bytes 484
  84.0 161.9 %copy-start.19 = (f32[40]{0:T(128)S(1)}, f32[40]{0:T(128)}, u32[]{:S(2)}) copy-start(f32[40]{0:T(128)} %param.38) | copy-start | bytes 484
  84.0 161.9 %copy-start.20 = (f32[40]{0:T(128)S(1)}, f32[40]{0:T(128)}, u32[]{:S(2)}) copy-start(f32[40]{0:T(128)} %param.46) | copy-start | bytes 484
  84.0 164.8 %copy-start.7 = (f32[160,40]{0,1:T(8,128)S(1)}, f32[160,40]{0,1:T(8,128)}, u32[]{:S(2)}) copy-start(f32[160,40]{0,1:T(8,128)} %param.37) | copy-start | bytes 76804
  84.0 164.8 %copy-start.8 = (f32[160,40]{0,1:T(8,128)S(1)}, f32[160,40]{0,1:T(8,128)}, u32[]{:S(2)}) copy-start(f32[160,40]{0,1:T(8,128)} %param.45) | copy-start | bytes 76804
  84.1 165.5 %copy-start.9 = (f32[40,160]{1,0:T(8,128)S(1)}, f32[40,160]{1,0:T(8,128)}, u32[]{:S(2)}) copy-start(f32[40,160]{1,0:T(8,128)} %param.34) | copy-start | bytes 76804
  84.1 165.4 %copy-start.10 = (f32[40,160]{1,0:T(8,128)S(1)}, f32[40,160]{1,0:T(8,128)}, u32[]{:S(2)}) copy-start(f32[40,160]{1,0:T(8,128)} %param.42) | copy-start | bytes 76804
  84.1 166.1 %copy-start.3 = (f32[640,40]{0,1:T(8,128)S(1)}, f32[640,40]{0,1:T(8,128)}, u32[]{:S(2)}) copy-start(f32[640,40]{0,1:T(8,128)} %param.33) | copy-start | bytes 307204
  84.1 166.1 %copy-start.4 = (f32[640,40]{0,1:T(8,128)S(1)}, f32[640,40]{0,1:T(8,128)}, u32[]{:S(2)}) copy-start(f32[640,40]{0,1:T(8,128)} %param.41) | copy-start | bytes 307204
  84.1 166.8 %copy-start.5 = (f32[40,640]{1,0:T(8,128)S(1)}, f32[40,640]{1,0:T(8,128)}, u32[]{:S(2)}) copy-start(f32[40,640]{1,0:T(8,128)} %param.32) | copy-start | bytes 307204
  84.1 166.8 %copy-start.6 = (f32[40,640]{1,0:T(8,128)S(1)}, f32[40,640]{1,0:T(8,128)}, u32[]{:S(2)}) copy-start(f32[40,640]{1,0:T(8,128)} %param.40) | copy-start | bytes 307204
  84.1 167.5 %copy-start.11 = (f32[40,160]{1,0:T(8,128)S(1)}, f32[40,160]{1,0:T(8,128)}, u32[]{:S(2)}) copy-start(f32[40,160]{1,0:T(8,128)} %param.36) | copy-start | bytes 76804
  84.1 167.4 %copy-start.12 = (f32[40,160]{1,0:T(8,128)S(1)}, f32[40,160]{1,0:T(8,128)}, u32[]{:S(2)}) copy-start(f32[40,160]{1,0:T(8,128)} %param.44) | copy-start | bytes 76804
  84.2 167.4 %copy-start.13 = (f32[40,160]{1,0:T(8,128)S(1)}, f32[40,160]{1,0:T(8,128)}, u32[]{:S(2)}) copy-start(f32[40,160]{1,0:T(8,128)} %param.35) | copy-start | bytes 76804
  84.2 167.4 %copy-start.14 = (f32[40,160]{1,0:T(8,128)S(1)}, f32[40,160]{1,0:T(8,128)}, u32[]{:S(2)}) copy-start(f32[40,160]{1,0:T(8,128)} %param.43) | copy-start | bytes 76804
  84.2 262.2 %all-gather.2.cloned.1.call-start = ((), (), s32[]{:S(2)}) async-start(), calls=%async_computation.2 | async-start | bytes 5406720 | tf_op jit(solution)/shard_map/all_gather | solution.py:34
Sparse Core Ops, SparseCore 0:
  84.3 160.2 reduce-scatter.1
  253.2 93.1 all-gather.1
where the time goes:
time: 369 us; the launch traced here: 368 us
  waiting for transfers between devices  253 us (69%)
  local copies, waits for them, and re-layouts  93 us (25%)
  between operations  14.4 us (4%)
  other arithmetic  6.58 us (2%)
    reduce_scatter x1, waiting for transfers between devices, sum_together(): lax.psum_scatter(lines, axis, tiled=True).reshape(-1)  160 us
    all_gather x1, waiting for transfers between devices, turned_gather(): whole = lax.all_gather(both, axis, axis=0, tiled=True)  93.3 us
    unnamed x59, local copies, waits for them, and re-layouts  31.3 us
    reshape x2, local copies, waits for them, and re-layouts, sum_together(): lines = jnp.concatenate([b.reshape(peers, -1) for b in parts], axis=1)  13.8 us
    another operation x4, local copies, waits for them, and re-layouts, sum_together(): lines = jnp.concatenate([b.reshape(peers, -1) for b in parts], axis=1)  10.6 us
    transpose x2, local copies, waits for them, and re-layouts, in_blocks(): return jnp.moveaxis(parts, dim, 0)  9.01 us
    pad x1, local copies, waits for them, and re-layouts, sum_together(): jnp.pad(lines, ((0, 0), (0, extent * 128 - lines.shape[1])))  8.25 us
    reshape x1, local copies, waits for them, and re-layouts, sum_together(): jnp.pad(lines, ((0, 0), (0, extent * 128 - lines.shape[1])))  8.22 us
  transfers between devices with their start and end apart: 2, of which 2 were waited for; matrix products, arithmetic and copies ran while one was open for 0% of the time, Pallas kernels for 0%

commit v1 on v0

--- a/solution.py
+++ b/solution.py
@@ -31,7 +31,9 @@
     turned = [jnp.moveaxis(a, dim, 0) for a, dim in zip(arrays, dims)]
     widths = [t[0].size for t in turned]
     both = jnp.concatenate([t.reshape(-1, w) for t, w in zip(turned, widths)], axis=1)
-    whole = lax.all_gather(both, axis, axis=0, tiled=True)
+    whole = jnp.concatenate(
+        lax.all_to_all(jnp.stack([both] * lax.axis_size(axis)), axis, 0, 0), axis=0
+    )
     parts = jnp.split(whole, [sum(widths[:k]) for k in range(1, len(widths))], axis=1)
     return tuple(
         (

time: 369 us -> 403 us (1.092)
  blocking collectives: 0 us -> 129 us
  waiting for transfers between devices: 253 us -> 160 us
    all_to_all x0 -> x1, blocking collectives: none -> 129 us  [turned_gather(): lax.all_to_all(jnp.stack([both] * lax.axis_size(axis)), axis, 0, 0)]
    all_gather x1 -> x0, waiting for transfers between devices: 93.3 us -> none  [turned_gather(): whole = lax.all_gather(both, axis, axis=0, tiled=True)]
  transfers between devices with their start and end apart: 2 -> 1, of which waited for: 2 -> 1; matrix products, arithmetic and copies ran while one was open for 0% -> 0% of each run, Pallas kernels for 0% -> 0%
where the time goes in v1:
time: 403 us; the launch traced here: 401 us
  waiting for transfers between devices  160 us (40%)
  blocking collectives  129 us (32%)
  local copies, waits for them, and re-layouts  91.5 us (23%)
  between operations  14.4 us (4%)
  other arithmetic  6.57 us (2%)
    reduce_scatter x1, waiting for transfers between devices, sum_together(): lax.psum_scatter(lines, axis, tiled=True).reshape(-1)  160 us
    all_to_all x1, blocking collectives, turned_gather(): lax.all_to_all(jnp.stack([both] * lax.axis_size(axis)), axis, 0, 0)  129 us
    unnamed x59, local copies, waits for them, and re-layouts  33.6 us
    reshape x2, local copies, waits for them, and re-layouts, sum_together(): lines = jnp.concatenate([b.reshape(peers, -1) for b in parts], axis=1)  13.8 us
    another operation x4, local copies, waits for them, and re-layouts, sum_together(): lines = jnp.concatenate([b.reshape(peers, -1) for b in parts], axis=1)  10.6 us
    transpose x2, local copies, waits for them, and re-layouts, in_blocks(): return jnp.moveaxis(parts, dim, 0)  9.15 us
    pad x1, local copies, waits for them, and re-layouts, sum_together(): jnp.pad(lines, ((0, 0), (0, extent * 128 - lines.shape[1])))  8.25 us
    reshape x1, local copies, waits for them, and re-layouts, sum_together(): jnp.pad(lines, ((0, 0), (0, extent * 128 - lines.shape[1])))  8.24 us
  transfers between devices with their start and end apart: 1, of which 1 were waited for; matrix products, arithmetic and copies ran while one was open for 0% of the time, Pallas kernels for 0%

profile of v1, /device:TPU:1, one launch (start us, length us, event | category | flops | bytes accessed | tf_op | source)
XLA Modules:
  0.0 401.4 jit_solution(12864839686089982369)
XLA Ops:
  7.2 3.5 copy.89
  10.7 6.1 %copy.90 = f32[32,640,40]{2,1,0:T(8,128)} copy(f32[32,640,40]{1,2,0:T(8,128)S(1)} %bitcast.23) | data formatting | bytes 6553600 | tf_op jit(solution)/shard_map/transpose | solution.py:13
  16.8 10.0 %reshape.107 = f32[32,25600]{1,0:T(8,128)} reshape(f32[32,640,40]{2,1,0:T(8,128)} %copy.90) | data formatting | bytes 6553600 | tf_op jit(solution)/shard_map/reshape | solution.py:19
  26.8 2.2 reshape_reshape_squeeze.12
  29.0 1.9 constant_dynamic-update-slice_fusion.5
  31.0 2.6 copy.91
  33.6 2.9 reshape_reshape_squeeze.13
  36.5 2.6 copy.92
  39.1 2.8 reshape_reshape_squeeze.14
  41.8 2.6 copy.93
  44.4 2.8 reshape_reshape_squeeze.15
  47.2 2.6 copy.94
  49.8 3.0 copy.95
  52.9 3.8 reshape.108
  56.9 1.9 constant_dynamic-update-slice_fusion.4
  58.8 2.1 constant_dynamic-update-slice_fusion.3
  61.0 2.1 constant_dynamic-update-slice_fusion.2
  63.1 1.0 constant_dynamic-update-slice_fusion.1
  64.0 1.0 constant_dynamic-update-slice_fusion
  65.0 1.3 dynamic-update-slice.6
  66.4 1.4 dynamic-update-slice.7
  67.8 8.3 %pad.4 = f32[32,77824]{1,0:T(8,128)} pad(f32[32,76880]{1,0:T(8,128)} %dynamic-update-slice.7, f32[]{:T(128)} %constant.5.clone.1), padding=0_0x0_944 | pad | bytes 19802116 | tf_op jit(solution)/shard_map/jit(_pad)/pad | solution.py:21
  76.0 8.2 %reshape.109 = f32[19456,128]{1,0:T(8,128)} reshape(f32[32,77824]{1,0:T(8,128)} %pad.4) | data formatting | bytes 19922944 | tf_op jit(solution)/shard_map/reshape | solution.py:21
  84.4 160.4 %reduce-scatter.2.cloned.1.call-done = f32[608,128]{1,0:T(8,128)} async-done(((f32[19456,128]{1,0:T(8,128)}), f32[608,128]{1,0:T(8,128)}) %reduce-scatter.2.cloned.1.call-update) | async-done | bytes 311312 | tf_op jit(solution)/shard_map/reduce_scatter | solution.py:22
  244.8 0.8 slice_multiply_fusion.2
  245.8 0.1 mul.141
  246.1 1.3 convert_bitcast_fusion.2
  247.5 0.1 copy.98
  247.6 0.1 copy.99
  247.7 1.0 slice_multiply_fusion
  248.7 0.2 mul.123
  248.9 0.1 copy.96
  249.1 0.6 convert_bitcast_fusion.1
  249.7 0.6 fusion.6
  250.4 0.7 convert_bitcast_fusion
  251.1 0.7 fusion.7
  251.8 0.7 fusion.4
  252.5 0.1 concatenate.7
  252.6 0.6 stack.2
  253.3 128.6 %all_to_all.5 = bf16[32,40,1922]{2,1,0:T(8,128)(2,1)S(1)} all-to-all(bf16[32,40,1922]{2,1,0:T(8,128)(2,1)S(1)} %stack.2), channel_id=1, replica_groups=mesh['data'=32,'width'=8] {'data'}, dimensions={0} | all-to-all | bytes 9840640 | tf_op jit(solution)/shard_map/all_to_all | solution.py:35
  381.9 2.0 slice_bitcast_fusion.1
  383.9 1.5 slice_bitcast_fusion
  385.4 1.0 slice_reduce_fusion
  386.4 2.1 copy.101
  388.4 2.1 copy.102
  390.5 1.0 copy.103
  391.4 1.0 copy.104
  392.4 2.2 copy.100
  (53 shorter events, 0.7 us)
Async XLA Ops:
  7.2 237.6 %reduce-scatter.2.cloned.1.call-start = ((), (), s32[]{:S(2)}) async-start(), calls=%async_computation.2 | async-start | bytes 10272768 | tf_op jit(solution)/shard_map/reduce_scatter | solution.py:22
  33.6 23.1 %copy-start.15 = (f32[1,1280]{1,0:T(1,128)S(1)}, f32[1,1280]{1,0:T(1,128)}, u32[]{:S(2)}) copy-start(f32[1,1280]{1,0:T(1,128)} %param.30) | copy-start | bytes 15364
  33.6 23.2 %copy-start.16 = (f32[1,1280]{1,0:T(1,128)S(1)}, f32[1,1280]{1,0:T(1,128)}, u32[]{:S(2)}) copy-start(f32[1,1280]{1,0:T(1,128)} %param.31) | copy-start | bytes 15364
  33.6 23.3 %copy-start = (f32[32,25600]{1,0:T(8,128)S(1)}, f32[32,25600]{1,0:T(8,128)}, u32[]{:S(2)}) copy-start(f32[32,25600]{1,0:T(8,128)} %reshape.107) | copy-start | bytes 9830404
  56.9 6.2 %copy-start.1 = (f32[32,6400]{1,0:T(8,128)S(1)}, f32[32,6400]{1,0:T(8,128)}, u32[]{:S(2)}) copy-start(f32[32,6400]{1,0:T(8,128)} %reshape_reshape_squeeze.15) | copy-start | bytes 2457604
  56.9 7.1 %copy-start.2 = (f32[32,6400]{1,0:T(8,128)S(1)}, f32[32,6400]{1,0:T(8,128)}, u32[]{:S(2)}) copy-start(f32[32,6400]{1,0:T(8,128)} %reshape.108) | copy-start | bytes 2457604
  84.3 161.9 %copy-start.17 = (f32[40]{0:T(128)S(1)}, f32[40]{0:T(128)}, u32[]{:S(2)}) copy-start(f32[40]{0:T(128)} %param.39) | copy-start | bytes 484
  84.3 161.9 %copy-start.18 = (f32[40]{0:T(128)S(1)}, f32[40]{0:T(128)}, u32[]{:S(2)}) copy-start(f32[40]{0:T(128)} %param.47) | copy-start | bytes 484
  84.3 161.9 %copy-start.19 = (f32[40]{0:T(128)S(1)}, f32[40]{0:T(128)}, u32[]{:S(2)}) copy-start(f32[40]{0:T(128)} %param.38) | copy-start | bytes 484
  84.3 161.9 %copy-start.20 = (f32[40]{0:T(128)S(1)}, f32[40]{0:T(128)}, u32[]{:S(2)}) copy-start(f32[40]{0:T(128)} %param.46) | copy-start | bytes 484
  84.3 164.8 %copy-start.7 = (f32[160,40]{0,1:T(8,128)S(1)}, f32[160,40]{0,1:T(8,128)}, u32[]{:S(2)}) copy-start(f32[160,40]{0,1:T(8,128)} %param.37) | copy-start | bytes 76804
  84.3 164.8 %copy-start.8 = (f32[160,40]{0,1:T(8,128)S(1)}, f32[160,40]{0,1:T(8,128)}, u32[]{:S(2)}) copy-start(f32[160,40]{0,1:T(8,128)} %param.45) | copy-start | bytes 76804
  84.3 165.4 %copy-start.9 = (f32[40,160]{1,0:T(8,128)S(1)}, f32[40,160]{1,0:T(8,128)}, u32[]{:S(2)}) copy-start(f32[40,160]{1,0:T(8,128)} %param.34) | copy-start | bytes 76804
  84.3 165.4 %copy-start.10 = (f32[40,160]{1,0:T(8,128)S(1)}, f32[40,160]{1,0:T(8,128)}, u32[]{:S(2)}) copy-start(f32[40,160]{1,0:T(8,128)} %param.42) | copy-start | bytes 76804
  84.3 166.1 %copy-start.3 = (f32[640,40]{0,1:T(8,128)S(1)}, f32[640,40]{0,1:T(8,128)}, u32[]{:S(2)}) copy-start(f32[640,40]{0,1:T(8,128)} %param.33) | copy-start | bytes 307204
  84.3 166.1 %copy-start.4 = (f32[640,40]{0,1:T(8,128)S(1)}, f32[640,40]{0,1:T(8,128)}, u32[]{:S(2)}) copy-start(f32[640,40]{0,1:T(8,128)} %param.41) | copy-start | bytes 307204
  84.3 166.8 %copy-start.5 = (f32[40,640]{1,0:T(8,128)S(1)}, f32[40,640]{1,0:T(8,128)}, u32[]{:S(2)}) copy-start(f32[40,640]{1,0:T(8,128)} %param.32) | copy-start | bytes 307204
  84.4 166.8 %copy-start.6 = (f32[40,640]{1,0:T(8,128)S(1)}, f32[40,640]{1,0:T(8,128)}, u32[]{:S(2)}) copy-start(f32[40,640]{1,0:T(8,128)} %param.40) | copy-start | bytes 307204
  84.4 167.4 %copy-start.11 = (f32[40,160]{1,0:T(8,128)S(1)}, f32[40,160]{1,0:T(8,128)}, u32[]{:S(2)}) copy-start(f32[40,160]{1,0:T(8,128)} %param.36) | copy-start | bytes 76804
  84.4 167.4 %copy-start.12 = (f32[40,160]{1,0:T(8,128)S(1)}, f32[40,160]{1,0:T(8,128)}, u32[]{:S(2)}) copy-start(f32[40,160]{1,0:T(8,128)} %param.44) | copy-start | bytes 76804
  84.4 167.4 %copy-start.13 = (f32[40,160]{1,0:T(8,128)S(1)}, f32[40,160]{1,0:T(8,128)}, u32[]{:S(2)}) copy-start(f32[40,160]{1,0:T(8,128)} %param.35) | copy-start | bytes 76804
  84.4 167.4 %copy-start.14 = (f32[40,160]{1,0:T(8,128)S(1)}, f32[40,160]{1,0:T(8,128)}, u32[]{:S(2)}) copy-start(f32[40,160]{1,0:T(8,128)} %param.43) | copy-start | bytes 76804
Sparse Core Ops, SparseCore 0:
  84.6 160.2 reduce-scatter.1
